TPU v7x, 16 devices: a whole 2x2x2 slice. The times are simulated.
16 devices in a mesh: tp: 2 (over z), dp: 8 (over y, x, core).
Axes of the slice: x: 2, y: 2, z: 2, core: 2. Of those that a mesh axis runs over, the one named last changes fastest.
Arguments:
- x_in: bfloat16 [128, 3072], P(('dp', 'tp'))
- w_gate: bfloat16 [3072, 24576], P('dp', 'tp')
- w_up: bfloat16 [3072, 24576], P('dp', 'tp')
- w_down: bfloat16 [24576, 3072], P('tp', 'dp')
- grad_y: bfloat16 [128, 3072], P(('dp', 'tp'))
Outputs:
- output 1: bfloat16 [128, 3072], P(('dp', 'tp'))
- output 2: bfloat16 [128, 3072], P(('dp', 'tp'))
- output 3: float32 [3072, 24576], P('dp', 'tp')
- output 4: float32 [3072, 24576], P('dp', 'tp')
- output 5: float32 [24576, 3072], P('tp', 'dp')
All inputs are finite; a program needn't handle non-finite values.
Results may differ from a plain program's by a relative error of at most 0.0018.
Values are sent between devices in bfloat16 or wider.
A program may use at most 1 GiB of HBM per device.

v0:
```python
import jax
import jax.numpy as jnp
from jax import lax
from jax.sharding import PartitionSpec as P


def solution(mesh):
    dp_size = mesh.shape["dp"]
    tp_size = mesh.shape["tp"]

    def spread_cols(rows_loc):
        tok_dev = rows_loc.shape[0]
        cols_mine = lax.all_to_all(rows_loc, "dp", 1, 0, tiled=True)
        col_width = cols_mine.shape[1]
        cols_mine = cols_mine.reshape(dp_size, tok_dev, col_width)
        gathered = lax.all_gather(cols_mine, "tp", axis=1)
        return cols_mine, gathered.reshape(dp_size * tp_size * tok_dev, col_width)

    def collect_rows(col_part, resid):
        tok_dev = resid.shape[1]
        col_width = col_part.shape[1]
        summed = lax.psum_scatter(col_part.reshape(dp_size, tp_size, tok_dev, col_width), "tp", scatter_dimension=1, tiled=True)
        summed = summed.reshape(dp_size, tok_dev, col_width) + resid.astype(jnp.float32)
        out_rows = lax.all_to_all(summed.astype(jnp.bfloat16), "dp", 0, 2, tiled=True)
        return out_rows.reshape(tok_dev, dp_size * col_width)

    def local_step(x_loc, wg_loc, wu_loc, wd_loc, gy_loc):
        x_mine, x_cols = spread_cols(x_loc)
        gate_pre = lax.psum_scatter(jnp.dot(x_cols, wg_loc, preferred_element_type=jnp.float32), "dp", scatter_dimension=0, tiled=True)
        up_pre = lax.psum_scatter(jnp.dot(x_cols, wu_loc, preferred_element_type=jnp.float32), "dp", scatter_dimension=0, tiled=True)
        sig_gate = jax.nn.sigmoid(gate_pre)
        silu_gate = gate_pre * sig_gate
        hidden = (silu_gate * up_pre).astype(jnp.bfloat16)
        hidden_all = lax.all_gather(hidden, "dp", axis=0, tiled=True)
        y_rows = collect_rows(jnp.dot(hidden_all, wd_loc, preferred_element_type=jnp.float32), x_mine)

        gy_mine, gy_cols = spread_cols(gy_loc)
        grad_h = lax.psum_scatter(jnp.einsum("nd,fd->nf", gy_cols, wd_loc, preferred_element_type=jnp.float32), "dp", scatter_dimension=0, tiled=True)
        grad_wd = jnp.einsum("nf,nd->fd", hidden_all, gy_cols, preferred_element_type=jnp.float32)
        silu_deriv = sig_gate * (1.0 + gate_pre * (1.0 - sig_gate))
        grad_gate = (grad_h * up_pre * silu_deriv).astype(jnp.bfloat16)
        grad_up = (grad_h * silu_gate).astype(jnp.bfloat16)
        gate_all = lax.all_gather(grad_gate, "dp", axis=0, tiled=True)
        up_all = lax.all_gather(grad_up, "dp", axis=0, tiled=True)
        grad_wg = jnp.einsum("nd,nf->df", x_cols, gate_all, preferred_element_type=jnp.float32)
        grad_wu = jnp.einsum("nd,nf->df", x_cols, up_all, preferred_element_type=jnp.float32)
        gx_part = (jnp.einsum("nf,df->nd", gate_all, wg_loc, preferred_element_type=jnp.float32)
                   + jnp.einsum("nf,df->nd", up_all, wu_loc, preferred_element_type=jnp.float32))
        gx_rows = collect_rows(gx_part, gy_mine)
        return y_rows, gx_rows, grad_wg, grad_wu, grad_wd

    row_spec = P(("dp", "tp"), None)
    up_spec = P("dp", "tp")
    down_spec = P("tp", "dp")
    return jax.shard_map(local_step, mesh=mesh,
                         in_specs=(row_spec, up_spec, up_spec, down_spec, row_spec),
                         out_specs=(row_spec, row_spec, up_spec, up_spec, down_spec),
                         check_vma=False)
```

profile of v0, /device:TPU:0, one launch (start us, length us, event | category | flops | bytes accessed | tf_op | source)
XLA Modules:
  0.0 398.2 jit_solution(9495911039963117037)
XLA Ops:
  7.2 10.4 %all_to_all.62 = bf16[8,8,384]{2,0,1:T(8,128)(2,1)S(1)} all-to-all(bf16[8,8,384]{2,0,1:T(8,128)(2,1)} %bitcast.71), channel_id=1, replica_groups=mesh['tp'=2,'dp'=8] {'dp'}, dimensions={1} | all-to-all | bytes 98304 | tf_op jit(solution)/shard_map/all_to_all | solution.py:13
  17.6 0.6 copy-done.3
  18.2 4.7 %all-gather = bf16[8,16,384]{2,1,0:T(8,128)(2,1)S(1)} all-gather(bf16[8,8,384]{2,1,0:T(8,128)(2,1)S(1)} %bitcast.67), channel_id=2, replica_groups=mesh['tp'=2,'dp'=8] {'tp'}, dimensions={1}, use_global_device_ids=true | all-gather | bytes 147456 | tf_op jit(solution)/shard_map/all_gather | solution.py:16
  22.9 8.2 %fusion.5 = f32[128,12288]{1,0:T(8,128)} fusion(bf16[128,384]{1,0:T(8,128)(2,1)S(1)} %bitcast.59, bf16[384,12288]{1,0:T(8,128)(2,1)} %param.6), kind=kOutput, calls=%fused_computation.14 | convolution fusion | flops 1207959552 | bytes 15826944 | tf_op jit(solution)/shard_map/dot_general | solution.py:29
  31.2 9.1 %fusion.6 = f32[128,12288]{1,0:T(8,128)} fusion(bf16[128,384]{1,0:T(8,128)(2,1)S(1)} %bitcast.60, bf16[384,12288]{1,0:T(8,128)(2,1)} %param.7), kind=kOutput, calls=%fused_computation.15 | convolution fusion | flops 1207959552 | bytes 15826944 | tf_op jit(solution)/shard_map/dot_general | solution.py:30
  40.4 7.3 %all_to_all.63 = bf16[8,8,384]{2,0,1:T(8,128)(2,1)S(1)} all-to-all(bf16[8,8,384]{2,0,1:T(8,128)(2,1)S(1)} %bitcast.72), channel_id=1, replica_groups=mesh['tp'=2,'dp'=8] {'dp'}, dimensions={1} | all-to-all | bytes 98304 | tf_op jit(solution)/shard_map/all_to_all | solution.py:13
  48.3 4.7 %all-gather.1 = bf16[8,16,384]{2,1,0:T(8,128)(2,1)S(1)} all-gather(bf16[8,8,384]{2,1,0:T(8,128)(2,1)S(1)} %bitcast.68), channel_id=3, replica_groups=mesh['tp'=2,'dp'=8] {'tp'}, dimensions={1}, use_global_device_ids=true | all-gather | bytes 147456 | tf_op jit(solution)/shard_map/all_gather | solution.py:16
  53.1 9.4 %fusion.8 = f32[128,12288]{1,0:T(8,128)} fusion(bf16[128,384]{1,0:T(8,128)(2,1)S(1)} %bitcast.63, bf16[12288,384]{1,0:T(8,128)(2,1)} %param.8), kind=kOutput, calls=%fused_computation.17 | convolution fusion | flops 1207959552 | bytes 15826944 | tf_op jit(solution)/shard_map/nd,fd->nf/dot_general | solution.py:38
  62.6 24.1 %reduce-scatter.6.cloned.1.call-done = f32[16,12288]{1,0:T(8,128)} async-done(((f32[128,12288]{1,0:T(8,128)}), f32[16,12288]{1,0:T(8,128)}) %reduce-scatter.6.cloned.1.call-update) | async-done | bytes 786448 | tf_op jit(solution)/shard_map/reduce_scatter | solution.py:29
  86.7 60.1 %reduce-scatter.8.cloned.1.call-done = f32[16,12288]{1,0:T(8,128)} async-done(((f32[128,12288]{1,0:T(8,128)}), f32[16,12288]{1,0:T(8,128)}) %reduce-scatter.8.cloned.1.call-update) | async-done | bytes 786448 | tf_op jit(solution)/shard_map/reduce_scatter | solution.py:30
  146.7 60.1 %reduce-scatter.10.cloned.1.call-done = f32[16,12288]{1,0:T(8,128)} async-done(((f32[128,12288]{1,0:T(8,128)}), f32[16,12288]{1,0:T(8,128)}) %reduce-scatter.10.cloned.1.call-update) | async-done | bytes 786448 | tf_op jit(solution)/shard_map/reduce_scatter | solution.py:38
  206.8 2.9 multiply_convert_fusion
  211.2 0.7 dynamic-slice
  211.9 26.6 %all-gather.8.cloned.1.call-done = bf16[128,12288]{1,0:T(8,128)(2,1)} async-done(((bf16[16,12288]{1,0:T(8,128)(2,1)}), bf16[128,12288]{1,0:T(8,128)(2,1)}) %all-gather.8.cloned.1.call-update) | async-done | bytes 3145744 | tf_op jit(solution)/shard_map/all_gather | solution.py:43
  238.4 7.5 %fusion.9 = f32[128,384]{1,0:T(8,128)S(1)} fusion(bf16[128,12288]{1,0:T(8,128)(2,1)} %all-gather.8.cloned.1.call-done, bf16[384,12288]{1,0:T(8,128)(2,1)} %param.6), kind=kOutput, calls=%fused_computation.18 | convolution fusion | flops 1207959552 | bytes 12779520 | tf_op jit(solution)/shard_map/nf,df->nd/dot_general | solution.py:47
  246.0 23.2 %all-gather.6.cloned.1.call-done = bf16[128,12288]{1,0:T(8,128)(2,1)} async-done(((bf16[16,12288]{1,0:T(8,128)(2,1)}), bf16[128,12288]{1,0:T(8,128)(2,1)}) %all-gather.6.cloned.1.call-update) | async-done | bytes 3145744 | tf_op jit(solution)/shard_map/all_gather | solution.py:34
  269.2 7.1 %fusion.7 = f32[128,384]{1,0:T(8,128)} fusion(bf16[128,12288]{1,0:T(8,128)(2,1)} %all-gather.6.cloned.1.call-done, bf16[12288,384]{1,0:T(8,128)(2,1)} %param.8), kind=kOutput, calls=%fused_computation.16 | convolution fusion | flops 1207959552 | bytes 12779520 | tf_op jit(solution)/shard_map/dot_general | solution.py:35
  276.3 23.6 %all-gather.10.cloned.1.call-done = bf16[128,12288]{1,0:T(8,128)(2,1)} async-done(((bf16[16,12288]{1,0:T(8,128)(2,1)}), bf16[128,12288]{1,0:T(8,128)(2,1)}) %all-gather.10.cloned.1.call-update) | async-done | bytes 3145744 | tf_op jit(solution)/shard_map/all_gather | solution.py:44
  299.9 8.2 %convolution_add_fusion = f32[128,384]{1,0:T(8,128)} fusion(f32[128,384]{1,0:T(8,128)S(1)} %fusion.9, bf16[128,12288]{1,0:T(8,128)(2,1)} %all-gather.10.cloned.1.call-done, bf16[384,12288]{1,0:T(8,128)(2,1)} %param.7), kind=kOutput, calls=%fused_computation.2 | convolution fusion | flops 1208008704 | bytes 12976128 | tf_op jit(solution)/shard_map/nf,df->nd/dot_general | solution.py:48
  308.2 8.3 %convolution_bitcast_fusion.1 = f32[384,12288]{0,1:T(8,128)} fusion(bf16[128,12288]{1,0:T(8,128)(2,1)S(1)} %copy-done.1, bf16[128,384]{1,0:T(8,128)(2,1)S(1)} %bitcast.61), kind=kOutput, calls=%fused_computation.1 | convolution fusion | flops 1207959552 | bytes 22118400 | tf_op jit(solution)/shard_map/nd,nf->df/dot_general | solution.py:45
  316.5 8.0 %convolution_bitcast_fusion = f32[384,12288]{0,1:T(8,128)} fusion(bf16[128,12288]{1,0:T(8,128)(2,1)S(1)} %copy-done.2, bf16[128,384]{1,0:T(8,128)(2,1)S(1)} %bitcast.62), kind=kOutput, calls=%fused_computation | convolution fusion | flops 1207959552 | bytes 22118400 | tf_op jit(solution)/shard_map/nd,nf->df/dot_general | solution.py:46
  324.5 5.9 %all-reduce.5.cloned.1.call-done = (f32[8,2,8,384]{3,2,1,0:T(8,128)}, f32[8,2,8,384]{3,2,1,0:T(8,128)}) async-done(((f32[8,2,8,384]{3,2,1,0:T(8,128)}, f32[8,2,8,384]{3,2,1,0:T(8,128)}), (f32[8,2,8,384]{3,2,1,0:T(8,128)}, f32[8,2,8,384]{3,2,1,0:T(8,128)})) %all-reduce.5.cloned.1.call-update) | async-done | bytes 393232
  330.4 2.2 fusion.2
  332.6 3.6 all-to-all-start.3
  336.2 2.2 fusion.4
  338.4 2.7 all-to-all-done.3
  341.2 3.3 all-to-all-start.1
  344.5 8.3 %fusion.10 = f32[12288,384]{1,0:T(8,128)} fusion(bf16[128,12288]{1,0:T(8,128)(2,1)S(1)} %copy-done, bf16[128,384]{1,0:T(8,128)(2,1)S(1)} %bitcast.64), kind=kOutput, calls=%fused_computation.19 | convolution fusion | flops 1207959552 | bytes 22118400 | tf_op jit(solution)/shard_map/nf,nd->fd/dot_general | solution.py:39
  352.8 18.6 %copy.12 = f32[384,12288]{1,0:T(8,128)} copy(f32[384,12288]{0,1:T(8,128)} %convolution_bitcast_fusion.1) | data formatting | bytes 37748736
  371.5 18.7 %copy.13 = f32[384,12288]{1,0:T(8,128)} copy(f32[384,12288]{0,1:T(8,128)} %convolution_bitcast_fusion) | data formatting | bytes 37748736
  390.1 0.6 copy.22
  390.7 0.6 copy.23
  (32 shorter events, 2.3 us)
Async XLA Ops:
  7.2 79.5 %reduce-scatter.6.cloned.1.call-start = ((), (), s32[]{:S(2)}) async-start(), calls=%async_computation.7 | async-start | bytes 7077888 | tf_op jit(solution)/shard_map/reduce_scatter | solution.py:29
  17.6 0.6 copy-start.3
  31.2 9.2 %copy-start.7 = (bf16[8,3072]{1,0:T(8,128)(2,1)S(1)}, bf16[8,3072]{1,0:T(8,128)(2,1)}, u32[]{:S(2)}) copy-start(bf16[8,3072]{1,0:T(8,128)(2,1)} %param.9) | copy-start | bytes 147460
  31.2 115.6 %reduce-scatter.8.cloned.1.call-start = ((), (), s32[]{:S(2)}) async-start(), calls=%async_computation.8 | async-start | bytes 7077888 | tf_op jit(solution)/shard_map/reduce_scatter | solution.py:30
  40.3 166.5 %reduce-scatter.10.cloned.1.call-start = ((), (), s32[]{:S(2)}) async-start(), calls=%async_computation.10 | async-start | bytes 7077888 | tf_op jit(solution)/shard_map/reduce_scatter | solution.py:38
  47.7 0.6 copy-start.5
  62.5 148.7 %copy-start.8 = (u32[16]{0:T(128)S(1)}, u32[16]{0:T(128)}, u32[]{:S(2)}) copy-start(u32[16]{0:T(128)} %constant.6) | copy-start | bytes 196
  62.5 175.9 %all-gather.8.cloned.1.call-start = ((), (), s32[]{:S(2)}) async-start(), calls=%async_computation.11 | async-start | bytes 3538944 | tf_op jit(solution)/shard_map/all_gather | solution.py:43
  209.8 59.4 %all-gather.6.cloned.1.call-start = ((), (), s32[]{:S(2)}) async-start(), calls=%async_computation.9 | async-start | bytes 3538944 | tf_op jit(solution)/shard_map/all_gather | solution.py:34
  210.4 89.5 %all-gather.10.cloned.1.call-start = ((), (), s32[]{:S(2)}) async-start(), calls=%async_computation.12 | async-start | bytes 3538944 | tf_op jit(solution)/shard_map/all_gather | solution.py:44
  211.0 119.4 %all-reduce.5.cloned.1.call-start = ((), (), s32[]{:S(2)}) async-start(), calls=%async_computation.13 | async-start | bytes 786432
  276.3 31.8 %copy-start.1 = (bf16[128,12288]{1,0:T(8,128)(2,1)S(1)}, bf16[128,12288]{1,0:T(8,128)(2,1)}, u32[]{:S(2)}) copy-start(bf16[128,12288]{1,0:T(8,128)(2,1)} %all-gather.8.cloned.1.call-done) | copy-start | bytes 9437188
  308.2 8.3 %copy-start.2 = (bf16[128,12288]{1,0:T(8,128)(2,1)S(1)}, bf16[128,12288]{1,0:T(8,128)(2,1)}, u32[]{:S(2)}) copy-start(bf16[128,12288]{1,0:T(8,128)(2,1)} %all-gather.10.cloned.1.call-done) | copy-start | bytes 9437188
  316.5 13.9 %copy-start.6 = (bf16[8,8,384]{2,0,1:T(8,128)(2,1)S(1)}, bf16[8,8,384]{2,0,1:T(8,128)(2,1)}, u32[]{:S(2)}) copy-start(bf16[8,8,384]{2,0,1:T(8,128)(2,1)} %copy-done.5) | copy-start | bytes 147460
  316.5 19.8 %copy-start.4 = (bf16[8,8,384]{2,0,1:T(8,128)(2,1)S(1)}, bf16[8,8,384]{2,0,1:T(8,128)(2,1)}, u32[]{:S(2)}) copy-start(bf16[8,8,384]{2,0,1:T(8,128)(2,1)} %copy-done.3) | copy-start | bytes 147460
  316.5 28.0 %copy-start = (bf16[128,12288]{1,0:T(8,128)(2,1)S(1)}, bf16[128,12288]{1,0:T(8,128)(2,1)}, u32[]{:S(2)}) copy-start(bf16[128,12288]{1,0:T(8,128)(2,1)} %all-gather.6.cloned.1.call-done) | copy-start | bytes 9437188
  332.6 8.6 %all-to-all-start.3 = ((bf16[8,8,384]{2,1,0:T(8,128)(2,1)}), bf16[8,8,384]{2,1,0:T(8,128)(2,1)S(1)}, u32[]{:S(2)}, u32[]{:S(2)}) async-start(bf16[8,8,384]{2,1,0:T(8,128)(2,1)} %fusion.2), calls=%async_computation.6 | async-start | bytes 98304 | tf_op jit(solution)/shard_map/all_to_all | solution.py:24
  341.2 49.0 %all-to-all-start.1 = ((bf16[8,8,384]{2,1,0:T(8,128)(2,1)}), bf16[8,8,384]{2,1,0:T(8,128)(2,1)S(1)}, u32[]{:S(2)}, u32[]{:S(2)}) async-start(bf16[8,8,384]{2,1,0:T(8,128)(2,1)} %fusion.4), calls=%async_computation.3 | async-start | bytes 98304 | tf_op jit(solution)/shard_map/all_to_all | solution.py:24
Sparse Core Ops, SparseCore 0:
  31.3 55.3 reduce-scatter.5
  90.6 56.1 reduce-scatter.7
  150.7 56.1 reduce-scatter.9
  209.9 28.4 all-gather.7
  240.7 28.4 all-gather.5
  271.4 28.4 all-gather.9
  308.3 22.0 all-reduce.4
where the time goes:
time: 399 us; the launch traced here: 398 us
  waiting for transfers between devices  227 us (57%)
  matrix products  74.2 us (19%)
  local copies, waits for them, and re-layouts  40.5 us (10%)
  blocking collectives  27.2 us (7%)
  between operations  14.2 us (4%)
  starting transfers between devices  7.45 us (2%)
  other arithmetic  7.37 us (2%)
    reduce_scatter x1, waiting for transfers between devices, local_step(): lax.psum_scatter(jnp.einsum('nd,fd->nf', gy_cols, wd_loc, preferred_eleme...  60.1 us
    reduce_scatter x1, waiting for transfers between devices, local_step(): lax.psum_scatter(jnp.dot(x_cols, wu_loc, preferred_element_type=jnp.float...  60.1 us
    unnamed x23, local copies, waits for them, and re-layouts  40.5 us
    all_gather x1, waiting for transfers between devices, local_step(): gate_all = lax.all_gather(grad_gate, 'dp', axis=0, tiled=True)  26.6 us
    reduce_scatter x1, waiting for transfers between devices, local_step(): lax.psum_scatter(jnp.dot(x_cols, wg_loc, preferred_element_type=jnp.float...  24.1 us
    all_gather x1, waiting for transfers between devices, local_step(): up_all = lax.all_gather(grad_up, 'dp', axis=0, tiled=True)  23.6 us
    all_gather x1, waiting for transfers between devices, local_step(): hidden_all = lax.all_gather(hidden, 'dp', axis=0, tiled=True)  23.2 us
    all_to_all x2, blocking collectives, spread_cols(): cols_mine = lax.all_to_all(rows_loc, 'dp', 1, 0, tiled=True)  17.7 us
  transfers between devices with their start and end apart: 9, of which 8 were waited for; matrix products, arithmetic and copies ran while one was open for 25% of the time, Pallas kernels for 0%

commit v1 on v0

v1 whole, which is shorter than its diff:
```python
import functools

import jax
import jax.numpy as jnp
from jax import lax
from jax.experimental import pallas as pl
from jax.experimental.pallas import tpu as pltpu
from jax.sharding import PartitionSpec as P

MESH = pl.DeviceIdType.MESH
BF = jnp.bfloat16
F32 = jnp.float32

D = 3072
FF_LOC = 12288
DL = 384
NP = 8
FC = FF_LOC // (2 * NP)
NSUB = 256


def _dot(a, b, ca, cb):
    return lax.dot_general(a, b, (((ca,), (cb,)), ((), ())), preferred_element_type=F32)


def comm_kernel(x_ref, gy_ref, wg_hbm, wu_hbm, wd_hbm,
                y_ref, gx_ref, xs_ref, g_hbm,
                wg, wu, wd, xin, part, rd, r2, r3, gat, acc, rz, ob, orx,
                w_sem, x_send, x_recv, d_send, d_recv, s2_send, s2_recv, s3_send, s3_recv,
                s4_send, s4_recv, s5_send, s5_recv, s6_send, s6_recv, g_sem,
                z_send, z_recv, o_send, o_recv):
    tp = lax.axis_index("tp")
    dp = lax.axis_index("dp")
    c = lax.rem(dp, 2)
    mx = lax.rem(dp // 2, 2)
    my = dp // 4

    def dpi(cc, yy, xx):
        return yy * 4 + xx * 2 + cc

    core_nb = (tp, dpi(1 - c, my, mx))
    x_nb = (tp, dpi(c, my, 1 - mx))
    y_nb = (tp, dpi(c, 1 - my, mx))
    z_nb = (1 - tp, dp)

    def w_copies(p):
        cols = pl.ds(pl.multiple_of(p * 2 * FC, 2 * FC), 2 * FC)
        return (pltpu.make_async_copy(wg_hbm.at[:, cols], wg.at[p], w_sem.at[0, p]),
                pltpu.make_async_copy(wu_hbm.at[:, cols], wu.at[p], w_sem.at[1, p]),
                pltpu.make_async_copy(wd_hbm.at[cols, :], wd.at[p], w_sem.at[2, p]))

    @pl.loop(0, NP)
    def _(p):
        for cp in w_copies(p):
            cp.start()

    barrier = pltpu.get_barrier_semaphore()
    me = tp * 8 + dp

    @pl.loop(1, 16)
    def _(k):
        o = lax.rem(me + k, 16)
        pl.semaphore_signal(barrier, inc=1, device_id=(o // 8, lax.rem(o, 8)), device_id_type=MESH)
    pl.semaphore_wait(barrier, 15)

    def blk(tt, dd):
        return (lax.rem(dd, 2) * 4 + (dd // 4) * 2 + lax.rem(dd // 2, 2)) * 2 + tt

    def x_copy(k, j):
        o = lax.rem(me + k, 16)
        ot, od = o // 8, lax.rem(o, 8)
        src = (x_ref, gy_ref)[j].at[:, pl.ds(pl.multiple_of(od * DL, DL), DL)]
        return pltpu.make_async_remote_copy(
            src_ref=src, dst_ref=xin.at[blk(tp, dp), j], send_sem=x_send.at[k, j],
            recv_sem=x_recv.at[blk(tp, dp), j], device_id=(ot, od), device_id_type=MESH)

    def x_wait(k, j):
        o = lax.rem(me + k, 16)
        ot, od = o // 8, lax.rem(o, 8)
        return pltpu.make_async_remote_copy(
            src_ref=x_ref.at[:, pl.ds(0, DL)], dst_ref=xin.at[blk(ot, od), j], send_sem=x_send.at[k, j],
            recv_sem=x_recv.at[blk(ot, od), j], device_id=(ot, od), device_id_type=MESH)

    @pl.loop(1, 16)
    def _(k):
        for j in range(2):
            x_copy(k, j).start()

    mine = blk(tp, dp)
    own = pl.ds(pl.multiple_of(dp * DL, DL), DL)
    xin[mine, 0] = x_ref[:, own]
    xin[mine, 1] = gy_ref[:, own]
    acc[...] = jnp.zeros_like(acc)

    @pl.loop(1, 16)
    def _(k):
        for j in range(2):
            x_wait(k, j).wait_recv()

    for j in range(2):
        xs_ref[j] = xin[:, j].astype(F32).reshape(128, DL).astype(BF)

    def d_copy(p):
        s = lax.rem(p, 2)
        return pltpu.make_async_remote_copy(
            src_ref=part.at[s, 1 - c], dst_ref=rd.at[p], send_sem=d_send.at[p], recv_sem=d_recv.at[p],
            device_id=core_nb, device_id_type=MESH)

    def s2_copies(p):
        return (pltpu.make_async_remote_copy(
                    src_ref=rd.at[p, 0, :, :, 1 - mx], dst_ref=r2.at[p, 0], send_sem=s2_send.at[0, p],
                    recv_sem=s2_recv.at[0, p], device_id=x_nb, device_id_type=MESH),
                pltpu.make_async_remote_copy(
                    src_ref=rd.at[p, 1, :, 1 - my], dst_ref=r2.at[p, 1], send_sem=s2_send.at[1, p],
                    recv_sem=s2_recv.at[1, p], device_id=y_nb, device_id_type=MESH))

    def s3_copies(p):
        return (pltpu.make_async_remote_copy(
                    src_ref=r2.at[p, 0, :, 1 - my], dst_ref=r3.at[p, 0], send_sem=s3_send.at[0, p],
                    recv_sem=s3_recv.at[0, p], device_id=y_nb, device_id_type=MESH),
                pltpu.make_async_remote_copy(
                    src_ref=r2.at[p, 1, :, 1 - mx], dst_ref=r3.at[p, 1], send_sem=s3_send.at[1, p],
                    recv_sem=s3_recv.at[1, p], device_id=x_nb, device_id_type=MESH))

    def s4_copies(p, yy0, xx1):
        return (pltpu.make_async_remote_copy(
                    src_ref=gat.at[p, 0, c, yy0, mx], dst_ref=gat.at[p, 0, c, yy0, mx],
                    send_sem=s4_send.at[0, p], recv_sem=s4_recv.at[0, p], device_id=y_nb, device_id_type=MESH),
                pltpu.make_async_remote_copy(
                    src_ref=gat.at[p, 1, c, my, xx1], dst_ref=gat.at[p, 1, c, my, xx1],
                    send_sem=s4_send.at[1, p], recv_sem=s4_recv.at[1, p], device_id=x_nb, device_id_type=MESH))

    def s5_copies(p, xx0, yy1):
        return (pltpu.make_async_remote_copy(
                    src_ref=gat.at[p, 0, c, :, xx0], dst_ref=gat.at[p, 0, c, :, xx0],
                    send_sem=s5_send.at[0, p], recv_sem=s5_recv.at[0, p], device_id=x_nb, device_id_type=MESH),
                pltpu.make_async_remote_copy(
                    src_ref=gat.at[p, 1, c, yy1], dst_ref=gat.at[p, 1, c, yy1],
                    send_sem=s5_send.at[1, p], recv_sem=s5_recv.at[1, p], device_id=y_nb, device_id_type=MESH))

    def s6_copy(p, cc):
        return pltpu.make_async_remote_copy(
            src_ref=gat.at[p, :, cc], dst_ref=gat.at[p, :, cc], send_sem=s6_send.at[p],
            recv_sem=s6_recv.at[p], device_id=core_nb, device_id_type=MESH)

    def g_copy(p):
        return pltpu.make_async_copy(gat.at[p], g_hbm.at[p], g_sem.at[p])

    def products(p):
        s = lax.rem(p, 2)
        for cp in w_copies(p):
            cp.wait()

        @pl.when(p >= 2)
        def _():
            d_copy(p - 2).wait_send()

        for ab in range(2):
            for n in range(FC // NSUB):
                lo = ab * FC + n * NSUB
                cols = pl.ds(lo, NSUB)
                dst = pl.ds(n * NSUB, NSUB)
                vals = (_dot(xs_ref[0], wg[p, :, cols], 1, 0),
                        _dot(xs_ref[0], wu[p, :, cols], 1, 0),
                        _dot(xs_ref[1], wd[p, cols, :], 1, 1))
                for t in range(3):
                    v = vals[t].reshape(2, 2, 2, 16, NSUB)
                    for cc in range(2):
                        part[s, cc, ab, t, :, :, :, dst] = v[cc]
        d_copy(p).start()

    def stage2(p):
        s = lax.rem(p, 2)
        d_copy(p).wait_recv()
        for ab in range(2):
            for t in range(3):
                rd[p, ab, t] = rd[p, ab, t] + part[s, c, ab, t]
        for cp in s2_copies(p):
            cp.start()

    def stage3(p):
        for cp in s2_copies(p):
            cp.wait_recv()
        for t in range(3):
            r2[p, 0, t] = r2[p, 0, t] + rd[p, 0, t, :, mx]
            r2[p, 1, t] = r2[p, 1, t] + rd[p, 1, t, my]
        for cp in s3_copies(p):
            cp.start()

    def stage4(p):
        for cp in s3_copies(p):
            cp.wait_recv()
        for ab in range(2):
            keep = my if ab == 0 else mx
            a = r3[p, ab, 0] + r2[p, ab, 0, keep]
            b = r3[p, ab, 1] + r2[p, ab, 1, keep]
            g = r3[p, ab, 2] + r2[p, ab, 2, keep]
            s = jax.nn.sigmoid(a)
            silu = a * s
            gat[p, ab, c, my, mx, 0] = (silu * b).astype(BF)
            gat[p, ab, c, my, mx, 1] = (g * b * (s * (1.0 + a * (1.0 - s)))).astype(BF)
            gat[p, ab, c, my, mx, 2] = (g * silu).astype(BF)
        for cp in s4_copies(p, my, mx):
            cp.start()

    def stage5(p):
        for cp in s4_copies(p, 1 - my, 1 - mx):
            cp.wait_recv()
        for cp in s5_copies(p, mx, my):
            cp.start()

    def stage6(p):
        for cp in s5_copies(p, 1 - mx, 1 - my):
            cp.wait_recv()
        s6_copy(p, c).start()

    def stage7(p):
        s6_copy(p, 1 - c).wait_recv()
        g_copy(p).start()
        for ab in range(2):
            cols = pl.ds(ab * FC, FC)
            h = gat[p, ab, :, :, :, 0].reshape(128, FC)
            acc[0] = acc[0] + _dot(h, wd[p, cols, :], 1, 0)
            da = gat[p, ab, :, :, :, 1].reshape(128, FC)
            db = gat[p, ab, :, :, :, 2].reshape(128, FC)
            acc[1] = acc[1] + (_dot(da, wg[p, :, cols], 1, 1) + _dot(db, wu[p, :, cols], 1, 1))

    products(0)

    @pl.loop(0, NP + 5)
    def _(i):
        pl.when(i < NP)(lambda: stage2(i))
        pl.when((i >= 1) & (i < NP + 1))(lambda: stage3(i - 1))
        pl.when((i >= 2) & (i < NP + 2))(lambda: stage4(i - 2))
        pl.when((i >= 3) & (i < NP + 3))(lambda: stage5(i - 3))
        pl.when((i >= 4) & (i < NP + 4))(lambda: stage6(i - 4))
        pl.when(i < NP - 1)(lambda: products(i + 1))
        pl.when(i >= 5)(lambda: stage7(i - 5))

    accv = acc.reshape(2, 8, 2, 8, DL)
    zc = pltpu.make_async_remote_copy(
        src_ref=accv.at[:, :, 1 - tp], dst_ref=rz, send_sem=z_send, recv_sem=z_recv,
        device_id=z_nb, device_id_type=MESH)
    zc.start()
    zc.wait_recv()
    for q in range(8):
        for j in range(2):
            tot = accv[j, q, tp] + rz[j, q] + xin[2 * q + tp, j].astype(F32)
            ob[q, j] = tot.astype(BF)

    def q_of(dd):
        return lax.rem(dd, 2) * 4 + (dd // 4) * 2 + lax.rem(dd // 2, 2)

    def o_copy(k, src_dp):
        od = lax.rem(dp + k, 8)
        return pltpu.make_async_remote_copy(
            src_ref=ob.at[q_of(od)], dst_ref=orx.at[src_dp], send_sem=o_send.at[k],
            recv_sem=o_recv.at[src_dp], device_id=(tp, od), device_id_type=MESH)

    @pl.loop(1, 8)
    def _(k):
        o_copy(k, dp).start()

    orx[dp] = ob[q_of(dp)]

    @pl.loop(0, NP)
    def _(p):
        for cp in (*s2_copies(p), *s3_copies(p), *s4_copies(p, my, mx), *s5_copies(p, mx, my), s6_copy(p, c)):
            cp.wait_send()
        g_copy(p).wait()
    for p in (NP - 2, NP - 1):
        d_copy(p).wait_send()

    @pl.loop(1, 16)
    def _(k):
        for j in range(2):
            x_copy(k, j).wait_send()
    zc.wait_send()

    @pl.loop(1, 8)
    def _(k):
        o_copy(k, lax.rem(dp + k, 8)).wait_recv()

    for dd in range(8):
        y_ref[:, dd * DL:(dd + 1) * DL] = orx[dd, 0]
        gx_ref[:, dd * DL:(dd + 1) * DL] = orx[dd, 1]

    @pl.loop(1, 8)
    def _(k):
        o_copy(k, dp).wait_send()


def wgrad_kernel(xs_ref, g_ref, dwg_ref, dwu_ref, dwd_ref):
    h = g_ref[0, 0, :, :, :, 0].reshape(128, FC)
    da = g_ref[0, 0, :, :, :, 1].reshape(128, FC)
    db = g_ref[0, 0, :, :, :, 2].reshape(128, FC)
    dwg_ref[...] = _dot(xs_ref[0], da, 0, 0)
    dwu_ref[...] = _dot(xs_ref[0], db, 0, 0)
    dwd_ref[...] = _dot(h, xs_ref[1], 0, 0)


def local_step(x_loc, wg_loc, wu_loc, wd_loc, gy_loc):
    vm = pl.BlockSpec(memory_space=pltpu.VMEM)
    hb = pl.BlockSpec(memory_space=pl.ANY)
    dma = pltpu.SemaphoreType.DMA
    y_rows, gx_rows, xs, gathered = pl.pallas_call(
        comm_kernel,
        out_shape=(jax.ShapeDtypeStruct((8, D), BF), jax.ShapeDtypeStruct((8, D), BF),
                   jax.ShapeDtypeStruct((2, 128, DL), BF),
                   jax.ShapeDtypeStruct((NP, 2, 2, 2, 2, 3, 16, FC), BF)),
        in_specs=[vm, vm, hb, hb, hb],
        out_specs=(vm, vm, vm, hb),
        scratch_shapes=[
            pltpu.VMEM((NP, DL, 2 * FC), BF),
            pltpu.VMEM((NP, DL, 2 * FC), BF),
            pltpu.VMEM((NP, 2 * FC, DL), BF),
            pltpu.VMEM((16, 2, 8, DL), BF),
            pltpu.VMEM((2, 2, 2, 3, 2, 2, 16, FC), F32),
            pltpu.VMEM((NP, 2, 3, 2, 2, 16, FC), F32),
            pltpu.VMEM((NP, 2, 3, 2, 16, FC), F32),
            pltpu.VMEM((NP, 2, 3, 16, FC), F32),
            pltpu.VMEM((NP, 2, 2, 2, 2, 3, 16, FC), BF),
            pltpu.VMEM((2, 128, DL), F32),
            pltpu.VMEM((2, 8, 8, DL), F32),
            pltpu.VMEM((8, 2, 8, DL), BF),
            pltpu.VMEM((8, 2, 8, DL), BF),
            dma((3, NP)), dma((16, 2)), dma((16, 2)), dma((NP,)), dma((NP,)),
            dma((2, NP)), dma((2, NP)), dma((2, NP)), dma((2, NP)),
            dma((2, NP)), dma((2, NP)), dma((2, NP)), dma((2, NP)),
            dma((NP,)), dma((NP,)), dma((NP,)),
            dma(()), dma(()), dma((8,)), dma((8,)),
        ],
        compiler_params=pltpu.CompilerParams(
            collective_id=0, has_side_effects=True, vmem_limit_bytes=60 * 1024 * 1024),
        name="mlp_comm",
    )(x_loc, gy_loc, wg_loc, wu_loc, wd_loc)

    grad_wg, grad_wu, grad_wd = pl.pallas_call(
        wgrad_kernel,
        grid=(2 * NP,),
        out_shape=(jax.ShapeDtypeStruct((DL, FF_LOC), F32), jax.ShapeDtypeStruct((DL, FF_LOC), F32),
                   jax.ShapeDtypeStruct((FF_LOC, DL), F32)),
        in_specs=[pl.BlockSpec((2, 128, DL), lambda k: (0, 0, 0)),
                  pl.BlockSpec((1, 1, 2, 2, 2, 3, 16, FC), lambda k: (k // 2, lax.rem(k, 2), 0, 0, 0, 0, 0, 0))],
        out_specs=(pl.BlockSpec((DL, FC), lambda k: (0, k)), pl.BlockSpec((DL, FC), lambda k: (0, k)),
                   pl.BlockSpec((FC, DL), lambda k: (k, 0))),
        compiler_params=pltpu.CompilerParams(dimension_semantics=("arbitrary",), vmem_limit_bytes=48 * 1024 * 1024),
        name="mlp_wgrad",
    )(xs, gathered)
    return y_rows, gx_rows, grad_wg, grad_wu, grad_wd


def solution(mesh):
    row_spec = P(("dp", "tp"), None)
    up_spec = P("dp", "tp")
    down_spec = P("tp", "dp")
    return jax.shard_map(local_step, mesh=mesh,
                         in_specs=(row_spec, up_spec, up_spec, down_spec, row_spec),
                         out_specs=(row_spec, row_spec, up_spec, up_spec, down_spec),
                         check_vma=False)
```

time: 399 us -> 172 us (0.43)
  waiting for transfers between devices: 227 us -> 0 us
  Pallas kernels: 0 us -> 168 us
  matrix products: 74.2 us -> 0 us
  local copies, waits for them, and re-layouts: 40.5 us -> 2.17 us
  blocking collectives: 27.2 us -> 0 us
  between operations: 14.2 us -> 0.65 us
  starting transfers between devices: 7.45 us -> 0 us
  other arithmetic: 7.37 us -> 0 us
    pallas_call x0 -> x2, Pallas kernels: none -> 168 us  [the longest x1 146 us: local_step(): pl.pallas_call(comm_kernel, out_shape=(jax.ShapeDtypeStruct((8, D), BF),...]
    reduce_scatter x3 -> x0, waiting for transfers between devices: 144 us -> none  [the longest x1 60.1 us: local_step(): lax.psum_scatter(jnp.einsum('nd,fd->nf', gy_cols, wd_loc, preferred_eleme...]
    dot_general x9 -> x0, matrix products: 74.2 us -> none  [the longest x1 9.41 us: local_step(): jnp.einsum('nd,fd->nf', gy_cols, wd_loc, preferred_element_type=jnp.float32)]
    all_gather x3 -> x0, waiting for transfers between devices: 73.4 us -> none  [the longest x1 26.6 us: local_step(): gate_all = lax.all_gather(grad_gate, 'dp', axis=0, tiled=True)]
    unnamed x23 -> x8, local copies, waits for them, and re-layouts: 40.5 us -> 2.17 us
    all_to_all x2 -> x0, blocking collectives: 17.7 us -> none  [spread_cols(): cols_mine = lax.all_to_all(rows_loc, 'dp', 1, 0, tiled=True)]
    all_gather x2 -> x0, blocking collectives: 9.49 us -> none  [spread_cols(): gathered = lax.all_gather(cols_mine, 'tp', axis=1)]
    convert_element_type x3 -> x0, other arithmetic: 7.37 us -> none  [the longest x2 4.43 us: collect_rows(): summed.astype(jnp.bfloat16)]
  transfers between devices with their start and end apart: 9 -> 0, of which waited for: 8 -> 0; matrix products, arithmetic and copies ran while one was open for 25% -> 0% of each run, Pallas kernels for 0% -> 0%
where the time goes in v1:
time: 172 us; the launch traced here: 171 us
  Pallas kernels  168 us (98%)
  local copies, waits for them, and re-layouts  2.17 us (1%)
    pallas_call x1, Pallas kernels, local_step(): pl.pallas_call(comm_kernel, out_shape=(jax.ShapeDtypeStruct((8, D), BF),...  146 us
    pallas_call x1, Pallas kernels, local_step(): pl.pallas_call(wgrad_kernel, grid=(2 * NP,), out_shape=(jax.ShapeDtypeStr...  22.2 us

profile of v1, /device:TPU:0, one launch (start us, length us, event | category | flops | bytes accessed | tf_op | source)
XLA Modules:
  0.0 170.9 jit_solution(17748813778087912988)
XLA Ops:
  0.6 145.8 %mlp_comm.1 = (bf16[8,3072]{1,0:T(8,128)(2,1)}, bf16[8,3072]{1,0:T(8,128)(2,1)}, bf16[2,128,384]{2,1,0:T(8,128)(2,1)}, bf16[8,2,2,2,2,3,16,768]{7,6,5,4,3,2,1,0:T(8,128)(2,1)}) custom-call(bf16[8,3072]{1,0:T(8,128)(2,1)} %x_ref.1, bf16[8,3072]{1,0:T(8,128)(2,1)} %gy_ref.1, bf16[384,12288]{1,0:T(8,128)(2,1)} %wg_hbm.1, bf16[384,12288]{1,0:T(8,128)(2,1)} %wu_hbm.1, ...), custom_call_target="tpu_custom_call" | custom-call | tf_op jit(solution)/shard_map/mlp_comm/pallas_call | solution.py:306
  146.5 0.0 copy-start
  146.5 0.9 copy-done
  147.4 0.0 copy-start.2
  147.4 0.0 copy-start.1
  147.4 22.2 %mlp_wgrad.1 = (f32[384,12288]{1,0:T(8,128)}, f32[384,12288]{1,0:T(8,128)}, f32[12288,384]{1,0:T(8,128)}) custom-call(bf16[2,128,384]{2,1,0:T(8,128)(2,1)S(1)} %copy-done, bf16[8,2,2,2,2,3,16,768]{7,6,5,4,3,2,1,0:T(8,128)(2,1)} %get-tuple-element.15.g_ref), custom_call_target="tpu_custom_call" | custom-call | tf_op jit(solution)/shard_map/mlp_wgrad/pallas_call | solution.py:338
  169.6 0.0 copy-done.2
  169.6 0.6 copy.12
  170.2 0.0 copy-done.1
  170.3 0.6 copy.13
Async XLA Ops:
  146.5 0.9 copy-start
  147.4 22.2 %copy-start.2 = (bf16[8,3072]{1,0:T(8,128)(2,1)S(1)}, bf16[8,3072]{1,0:T(8,128)(2,1)}, u32[]{:S(2)}) copy-start(bf16[8,3072]{1,0:T(8,128)(2,1)} %get-tuple-element.24) | copy-start | bytes 147460
  147.4 22.8 %copy-start.1 = (bf16[8,3072]{1,0:T(8,128)(2,1)S(1)}, bf16[8,3072]{1,0:T(8,128)(2,1)}, u32[]{:S(2)}) copy-start(bf16[8,3072]{1,0:T(8,128)(2,1)} %get-tuple-element.25) | copy-start | bytes 147460

commit v2 on v1

--- a/solution.py
+++ b/solution.py
@@ -14,9 +14,9 @@
 D = 3072
 FF_LOC = 12288
 DL = 384
-NP = 8
+NP = 16
 FC = FF_LOC // (2 * NP)
-NSUB = 256
+NSUB = 384
 
 
 def _dot(a, b, ca, cb):

time: 172 us -> 179 us (1.041)
  Pallas kernels: 168 us -> 176 us
    pallas_call x1, Pallas kernels: 22.2 us -> 29.3 us  [local_step(): pl.pallas_call(wgrad_kernel, grid=(2 * NP,), out_shape=(jax.ShapeDtypeStr...]
where the time goes in v2:
time: 179 us; the launch traced here: 178 us
  Pallas kernels  176 us (98%)
  local copies, waits for them, and re-layouts  2.17 us (1%)
    pallas_call x1, Pallas kernels, local_step(): pl.pallas_call(comm_kernel, out_shape=(jax.ShapeDtypeStruct((8, D), BF),...  146 us
    pallas_call x1, Pallas kernels, local_step(): pl.pallas_call(wgrad_kernel, grid=(2 * NP,), out_shape=(jax.ShapeDtypeStr...  29.3 us

profile of v2, /device:TPU:0, one launch (start us, length us, event | category | flops | bytes accessed | tf_op | source)
XLA Modules:
  0.0 178.4 jit_solution(11621306299984368108)
XLA Ops:
  0.6 146.2 %mlp_comm.1 = (bf16[8,3072]{1,0:T(8,128)(2,1)}, bf16[8,3072]{1,0:T(8,128)(2,1)}, bf16[2,128,384]{2,1,0:T(8,128)(2,1)}, bf16[16,2,2,2,2,3,16,384]{7,6,5,4,3,2,1,0:T(8,128)(2,1)}) custom-call(bf16[8,3072]{1,0:T(8,128)(2,1)} %x_ref.1, bf16[8,3072]{1,0:T(8,128)(2,1)} %gy_ref.1, bf16[384,12288]{1,0:T(8,128)(2,1)} %wg_hbm.1, bf16[384,12288]{1,0:T(8,128)(2,1)} %wu_hbm.1, ...), custom_call_target="tpu_custom_call" | custom-call | tf_op jit(solution)/shard_map/mlp_comm/pallas_call | solution.py:306
  146.9 0.0 copy-start
  146.9 0.9 copy-done
  147.8 0.0 copy-start.2
  147.8 0.0 copy-start.1
  147.8 29.3 %mlp_wgrad.1 = (f32[384,12288]{1,0:T(8,128)}, f32[384,12288]{1,0:T(8,128)}, f32[12288,384]{1,0:T(8,128)}) custom-call(bf16[2,128,384]{2,1,0:T(8,128)(2,1)S(1)} %copy-done, bf16[16,2,2,2,2,3,16,384]{7,6,5,4,3,2,1,0:T(8,128)(2,1)} %get-tuple-element.15.g_ref), custom_call_target="tpu_custom_call" | custom-call | tf_op jit(solution)/shard_map/mlp_wgrad/pallas_call | solution.py:338
  177.1 0.0 copy-done.2
  177.1 0.6 copy.12
  177.8 0.0 copy-done.1
  177.8 0.6 copy.13
Async XLA Ops:
  146.9 0.9 copy-start
  147.8 29.4 %copy-start.2 = (bf16[8,3072]{1,0:T(8,128)(2,1)S(1)}, bf16[8,3072]{1,0:T(8,128)(2,1)}, u32[]{:S(2)}) copy-start(bf16[8,3072]{1,0:T(8,128)(2,1)} %get-tuple-element.24) | copy-start | bytes 147460
  147.8 30.0 %copy-start.1 = (bf16[8,3072]{1,0:T(8,128)(2,1)S(1)}, bf16[8,3072]{1,0:T(8,128)(2,1)}, u32[]{:S(2)}) copy-start(bf16[8,3072]{1,0:T(8,128)(2,1)} %get-tuple-element.25) | copy-start | bytes 147460

commit v3 on v1

v3 whole, which is shorter than its diff:
```python
import functools

import jax
import jax.numpy as jnp
from jax import lax
from jax.experimental import pallas as pl
from jax.experimental.pallas import tpu as pltpu
from jax.sharding import PartitionSpec as P

MESH = pl.DeviceIdType.MESH
BF = jnp.bfloat16
F32 = jnp.float32

D = 3072
FF_LOC = 12288
DL = 384
NP = 8
FC = FF_LOC // (2 * NP)
NS = 3
SUB = FC // NS


def _dot(a, b, ca, cb):
    return lax.dot_general(a, b, (((ca,), (cb,)), ((), ())), preferred_element_type=F32)


def comm_kernel(x_ref, gy_ref, wg_hbm, wu_hbm, wd_hbm,
                y_ref, gx_ref, xs_ref, g_hbm,
                wg, wu, wd, st, xin, part, rd, r2, r3, gat, acc, fin,
                w_sem, x_send, x_recv, d_send, d_recv, d0_send, d0_recv, s2_send, s2_recv, s20_send, s20_recv,
                s3_send, s3_recv, s4_send, s4_recv, s5_send, s5_recv, s5l_send, s5l_recv,
                s6_send, s6_recv, s6l_send, s6l_recv, g_sem, o_send, o_recv):
    tp = lax.axis_index("tp")
    dp = lax.axis_index("dp")
    c = lax.rem(dp, 2)
    mx = lax.rem(dp // 2, 2)
    my = dp // 4
    me = tp * 8 + dp
    last = NP - 1

    def dpi(cc, yy, xx):
        return yy * 4 + xx * 2 + cc

    core_nb = (tp, dpi(1 - c, my, mx))
    x_nb = (tp, dpi(c, my, 1 - mx))
    y_nb = (tp, dpi(c, 1 - my, mx))

    def remote(src, dst, send, recv, dev):
        return pltpu.make_async_remote_copy(src_ref=src, dst_ref=dst, send_sem=send, recv_sem=recv,
                                            device_id=dev, device_id_type=MESH)

    def w_copies(p):
        cols = pl.ds(pl.multiple_of(p * 2 * FC, 2 * FC), 2 * FC)
        return (pltpu.make_async_copy(wg_hbm.at[:, cols], wg.at[p], w_sem.at[0, p]),
                pltpu.make_async_copy(wu_hbm.at[:, cols], wu.at[p], w_sem.at[1, p]),
                pltpu.make_async_copy(wd_hbm.at[cols, :], wd.at[p], w_sem.at[2, p]))

    barrier = pltpu.get_barrier_semaphore()

    def other(k):
        o = lax.rem(me + k, 16)
        return o // 8, lax.rem(o, 8)

    @pl.loop(1, 16)
    def _(k):
        pl.semaphore_signal(barrier, inc=1, device_id=other(k), device_id_type=MESH)

    @pl.loop(0, NP)
    def _(p):
        for cp in w_copies(p):
            cp.start()

    for dd in range(8):
        st[dd, 0] = x_ref[:, dd * DL:(dd + 1) * DL]
        st[dd, 1] = gy_ref[:, dd * DL:(dd + 1) * DL]
    acc[...] = jnp.zeros_like(acc)
    pl.semaphore_wait(barrier, 15)

    def blk(tt, dd):
        return (lax.rem(dd, 2) * 4 + (dd // 4) * 2 + lax.rem(dd // 2, 2)) * 2 + tt

    mine = blk(tp, dp)

    def x_copy(k, b):
        ot, od = other(k)
        return remote(st.at[od], xin.at[b], x_send.at[k], x_recv.at[b], (ot, od))

    @pl.loop(1, 16)
    def _(k):
        x_copy(k, mine).start()

    xin[mine] = st[dp]

    @pl.loop(1, 16)
    def _(k):
        x_copy(k, blk(*other(k))).wait_recv()

    for j in range(2):
        xs_ref[j] = xin[:, j].astype(F32).reshape(128, DL).astype(BF)

    def sub(n):
        return pl.ds(n * SUB, SUB)

    def d_copy(p, ab, n=None):
        s = lax.rem(p, 2)
        if n is None:
            return remote(part.at[s, 1 - c, ab], rd.at[p, ab], d_send.at[ab, p], d_recv.at[ab, p], core_nb)
        return remote(part.at[s, 1 - c, ab, :, :, :, :, sub(n)], rd.at[p, ab, :, :, :, :, sub(n)],
                      d0_send.at[ab, n], d0_recv.at[ab, n], core_nb)

    def s2_copy(p, ab, n=None):
        src = rd.at[p, 0, :, :, 1 - mx] if ab == 0 else rd.at[p, 1, :, 1 - my]
        dst = r2.at[p, ab]
        dev = x_nb if ab == 0 else y_nb
        if n is None:
            return remote(src, dst, s2_send.at[ab, p], s2_recv.at[ab, p], dev)
        return remote(src.at[:, :, :, sub(n)], dst.at[:, :, :, sub(n)], s20_send.at[ab, n], s20_recv.at[ab, n], dev)

    def s3_copies(p):
        return (remote(r2.at[p, 0, :, 1 - my], r3.at[p, 0], s3_send.at[0, p], s3_recv.at[0, p], y_nb),
                remote(r2.at[p, 1, :, 1 - mx], r3.at[p, 1], s3_send.at[1, p], s3_recv.at[1, p], x_nb))

    def s4_copies(p, yy0, xx1):
        b0, b1 = gat.at[p, 0, c, yy0, mx], gat.at[p, 1, c, my, xx1]
        return (remote(b0, b0, s4_send.at[0, p], s4_recv.at[0, p], y_nb),
                remote(b1, b1, s4_send.at[1, p], s4_recv.at[1, p], x_nb))

    def s5_copies(p, xx0, yy1, n=None):
        b0, b1 = gat.at[p, 0, c, :, xx0], gat.at[p, 1, c, yy1]
        if n is None:
            return (remote(b0, b0, s5_send.at[0, p], s5_recv.at[0, p], x_nb),
                    remote(b1, b1, s5_send.at[1, p], s5_recv.at[1, p], y_nb))
        b0, b1 = b0.at[:, :, :, sub(n)], b1.at[:, :, :, sub(n)]
        return (remote(b0, b0, s5l_send.at[0, n], s5l_recv.at[0, n], x_nb),
                remote(b1, b1, s5l_send.at[1, n], s5l_recv.at[1, n], y_nb))

    def s6_copy(p, cc, n=None):
        b = gat.at[p, :, cc]
        if n is None:
            return remote(b, b, s6_send.at[p], s6_recv.at[p], core_nb)
        b = b.at[:, :, :, :, :, sub(n)]
        return remote(b, b, s6l_send.at[n], s6l_recv.at[n], core_nb)

    def g_copy(p):
        return pltpu.make_async_copy(gat.at[p], g_hbm.at[p], g_sem.at[p])

    def product(p, ab, n):
        s = lax.rem(p, 2)
        cols = pl.ds(ab * FC + n * SUB, SUB)
        vals = (_dot(xs_ref[0], wg[p, :, cols], 1, 0),
                _dot(xs_ref[0], wu[p, :, cols], 1, 0),
                _dot(xs_ref[1], wd[p, cols, :], 1, 1))
        for t in range(3):
            v = vals[t].reshape(2, 2, 2, 16, SUB)
            for cc in range(2):
                part[s, cc, ab, t, :, :, :, sub(n)] = v[cc]

    def products(p):
        for cp in w_copies(p):
            cp.wait()
        for ab in range(2):
            @pl.when(p >= 3)
            def _():
                d_copy(p - 2, ab).wait_send()

            @pl.when(p == 2)
            def _():
                for n in range(NS):
                    d_copy(0, ab, n).wait_send()
            for n in range(NS):
                product(p, ab, n)
            d_copy(p, ab).start()

    def stage2(p):
        s = lax.rem(p, 2)
        for ab in range(2):
            d_copy(p, ab).wait_recv()
            for t in range(3):
                rd[p, ab, t] = rd[p, ab, t] + part[s, c, ab, t]
            s2_copy(p, ab).start()

    def stage3(p):
        for ab in range(2):
            @pl.when(p == 0)
            def _():
                for n in range(NS):
                    s2_copy(0, ab, n).wait_recv()

            @pl.when(p > 0)
            def _():
                s2_copy(p, ab).wait_recv()
            for t in range(3):
                r2[p, ab, t] = r2[p, ab, t] + (rd[p, 0, t, :, mx] if ab == 0 else rd[p, 1, t, my])
            s3_copies(p)[ab].start()

    def stage4(p):
        for ab in range(2):
            s3_copies(p)[ab].wait_recv()
            keep = my if ab == 0 else mx
            a = r3[p, ab, 0] + r2[p, ab, 0, keep]
            b = r3[p, ab, 1] + r2[p, ab, 1, keep]
            g = r3[p, ab, 2] + r2[p, ab, 2, keep]
            s = jax.nn.sigmoid(a)
            silu = a * s
            gat[p, ab, c, my, mx, 0] = (silu * b).astype(BF)
            gat[p, ab, c, my, mx, 1] = (g * b * (s * (1.0 + a * (1.0 - s)))).astype(BF)
            gat[p, ab, c, my, mx, 2] = (g * silu).astype(BF)
            s4_copies(p, my, mx)[ab].start()

    def stage5(p):
        for ab in range(2):
            s4_copies(p, 1 - my, 1 - mx)[ab].wait_recv()

            @pl.when(p < last)
            def _():
                s5_copies(p, mx, my)[ab].start()

            @pl.when(p == last)
            def _():
                for n in range(NS):
                    s5_copies(last, mx, my, n)[ab].start()

    def stage6(p):
        for cp in s5_copies(p, 1 - mx, 1 - my):
            cp.wait_recv()
        s6_copy(p, c).start()

    def accumulate(j, v):
        acc[j] = acc[j] + v.reshape(16, 8, DL)

    def y_part(p, lo, w):
        v = None
        for ab in range(2):
            h = gat[p, ab, :, :, :, 0, :, lo:lo + w].reshape(128, w)
            d = _dot(h, wd[p, ab * FC + lo:ab * FC + lo + w, :], 1, 0)
            v = d if v is None else v + d
        accumulate(0, v)

    def dx_part(p, lo, w):
        v = None
        for ab in range(2):
            for t, wt in ((1, wg), (2, wu)):
                z = gat[p, ab, :, :, :, t, :, lo:lo + w].reshape(128, w)
                d = _dot(z, wt[p, :, ab * FC + lo:ab * FC + lo + w], 1, 1)
                v = d if v is None else v + d
        accumulate(1, v)

    def stage7(p):
        s6_copy(p, 1 - c).wait_recv()
        g_copy(p).start()
        y_part(p, 0, FC)
        dx_part(p, 0, FC)

    for cp in w_copies(0):
        cp.wait()
    for n in range(NS):
        for ab in range(2):
            product(0, ab, n)
            d_copy(0, ab, n).start()
    for n in range(NS):
        for ab in range(2):
            d_copy(0, ab, n).wait_recv()
            rd[0, ab, :, :, :, :, sub(n)] = rd[0, ab, :, :, :, :, sub(n)] + part[0, c, ab, :, :, :, :, sub(n)]
            s2_copy(0, ab, n).start()

    @pl.loop(0, NP + 4)
    def _(i):
        pl.when((i >= 1) & (i < NP))(lambda: stage2(i))
        pl.when((i >= 1) & (i < NP + 1))(lambda: stage3(i - 1))
        pl.when((i >= 2) & (i < NP + 2))(lambda: stage4(i - 2))
        pl.when((i >= 3) & (i < NP + 3))(lambda: stage5(i - 3))
        pl.when((i >= 4) & (i < NP + 3))(lambda: stage6(i - 4))
        pl.when(i < NP - 1)(lambda: products(i + 1))
        pl.when(i >= 5)(lambda: stage7(i - 5))

    def o_copy(j, k, slot):
        ot, od = other(k)
        return remote(acc.at[j, blk(ot, od)], fin.at[j, slot], o_send.at[j, k], o_recv.at[j, slot], (ot, od))

    def send_out(j):
        @pl.loop(1, 16)
        def _(k):
            o_copy(j, k, me).start()
        fin[j, me] = acc[j, mine]

    for n in range(NS):
        for cp in s5_copies(last, 1 - mx, 1 - my, n):
            cp.wait_recv()
        s6_copy(last, c, n).start()
    for n in range(NS):
        s6_copy(last, 1 - c, n).wait_recv()
        if n == NS - 1:
            g_copy(last).start()
        y_part(last, n * SUB, SUB)
        if n == NS - 1:
            send_out(0)
        dx_part(last, n * SUB, SUB)
    send_out(1)

    @pl.loop(0, NP)
    def _(p):
        for cp in (*s3_copies(p), *s4_copies(p, my, mx)):
            cp.wait_send()
        g_copy(p).wait()

    @pl.loop(1, NP)
    def _(p):
        for ab in range(2):
            s2_copy(p, ab).wait_send()

    @pl.loop(0, NP - 1)
    def _(p):
        for cp in (*s5_copies(p, mx, my), s6_copy(p, c)):
            cp.wait_send()
    for n in range(NS):
        for ab in range(2):
            s2_copy(0, ab, n).wait_send()
            s5_copies(last, mx, my, n)[ab].wait_send()
        s6_copy(last, c, n).wait_send()
    for p in (NP - 2, NP - 1):
        for ab in range(2):
            d_copy(p, ab).wait_send()

    @pl.loop(1, 16)
    def _(k):
        x_copy(k, mine).wait_send()

    for j, (out, res) in enumerate(((y_ref, x_ref), (gx_ref, gy_ref))):
        @pl.loop(1, 16)
        def _(k):
            ot, od = other(k)
            o_copy(j, k, ot * 8 + od).wait_recv()
        for dd in range(8):
            cols = slice(dd * DL, (dd + 1) * DL)
            out[:, cols] = (res[:, cols].astype(F32) + (fin[j, dd] + fin[j, 8 + dd])).astype(BF)

    @pl.loop(1, 16)
    def _(k):
        for j in range(2):
            o_copy(j, k, me).wait_send()


def wgrad_kernel(xs_ref, g_ref, y_ref, gx_ref, yo_ref, gxo_ref, dwg_ref, dwu_ref, dwd_ref):
    @pl.when(pl.program_id(0) == 0)
    def _():
        yo_ref[...] = y_ref[...]
        gxo_ref[...] = gx_ref[...]
    h = g_ref[0, 0, :, :, :, 0].reshape(128, FC)
    da = g_ref[0, 0, :, :, :, 1].reshape(128, FC)
    db = g_ref[0, 0, :, :, :, 2].reshape(128, FC)
    dwg_ref[...] = _dot(xs_ref[0], da, 0, 0)
    dwu_ref[...] = _dot(xs_ref[0], db, 0, 0)
    dwd_ref[...] = _dot(h, xs_ref[1], 0, 0)


def local_step(x_loc, wg_loc, wu_loc, wd_loc, gy_loc):
    vm = pl.BlockSpec(memory_space=pltpu.VMEM)
    hb = pl.BlockSpec(memory_space=pl.ANY)
    dma = pltpu.SemaphoreType.DMA
    row = jax.ShapeDtypeStruct((8, D), BF)
    y_rows, gx_rows, xs, gathered = pl.pallas_call(
        comm_kernel,
        out_shape=(row, row, jax.ShapeDtypeStruct((2, 128, DL), BF),
                   jax.ShapeDtypeStruct((NP, 2, 2, 2, 2, 3, 16, FC), BF)),
        in_specs=[vm, vm, hb, hb, hb],
        out_specs=(vm, vm, vm, hb),
        scratch_shapes=[
            pltpu.VMEM((NP, DL, 2 * FC), BF),
            pltpu.VMEM((NP, DL, 2 * FC), BF),
            pltpu.VMEM((NP, 2 * FC, DL), BF),
            pltpu.VMEM((8, 2, 8, DL), BF),
            pltpu.VMEM((16, 2, 8, DL), BF),
            pltpu.VMEM((2, 2, 2, 3, 2, 2, 16, FC), F32),
            pltpu.VMEM((NP, 2, 3, 2, 2, 16, FC), F32),
            pltpu.VMEM((NP, 2, 3, 2, 16, FC), F32),
            pltpu.VMEM((NP, 2, 3, 16, FC), F32),
            pltpu.VMEM((NP, 2, 2, 2, 2, 3, 16, FC), BF),
            pltpu.VMEM((2, 16, 8, DL), F32),
            pltpu.VMEM((2, 16, 8, DL), F32),
            dma((3, NP)), dma((16,)), dma((16,)),
            dma((2, NP)), dma((2, NP)), dma((2, NS)), dma((2, NS)),
            dma((2, NP)), dma((2, NP)), dma((2, NS)), dma((2, NS)),
            dma((2, NP)), dma((2, NP)), dma((2, NP)), dma((2, NP)),
            dma((2, NP)), dma((2, NP)), dma((2, NS)), dma((2, NS)),
            dma((NP,)), dma((NP,)), dma((NS,)), dma((NS,)),
            dma((NP,)), dma((2, 16)), dma((2, 16)),
        ],
        compiler_params=pltpu.CompilerParams(
            collective_id=0, has_side_effects=True, vmem_limit_bytes=60 * 1024 * 1024),
        name="mlp_comm",
    )(x_loc, gy_loc, wg_loc, wu_loc, wd_loc)

    rows_spec = pl.BlockSpec((8, D), lambda k: (0, 0))
    return pl.pallas_call(
        wgrad_kernel,
        grid=(2 * NP,),
        out_shape=(row, row,
                   jax.ShapeDtypeStruct((DL, FF_LOC), F32), jax.ShapeDtypeStruct((DL, FF_LOC), F32),
                   jax.ShapeDtypeStruct((FF_LOC, DL), F32)),
        in_specs=[pl.BlockSpec((2, 128, DL), lambda k: (0, 0, 0)),
                  pl.BlockSpec((1, 1, 2, 2, 2, 3, 16, FC), lambda k: (k // 2, lax.rem(k, 2), 0, 0, 0, 0, 0, 0)),
                  rows_spec, rows_spec],
        out_specs=(rows_spec, rows_spec,
                   pl.BlockSpec((DL, FC), lambda k: (0, k)), pl.BlockSpec((DL, FC), lambda k: (0, k)),
                   pl.BlockSpec((FC, DL), lambda k: (k, 0))),
        compiler_params=pltpu.CompilerParams(dimension_semantics=("arbitrary",), vmem_limit_bytes=60 * 1024 * 1024),
        name="mlp_wgrad",
    )(xs, gathered, y_rows, gx_rows)


def solution(mesh):
    row_spec = P(("dp", "tp"), None)
    up_spec = P("dp", "tp")
    down_spec = P("tp", "dp")
    return jax.shard_map(local_step, mesh=mesh,
                         in_specs=(row_spec, up_spec, up_spec, down_spec, row_spec),
                         out_specs=(row_spec, row_spec, up_spec, up_spec, down_spec),
                         check_vma=False)
```

time: 172 us -> 164 us (0.953)
  Pallas kernels: 168 us -> 163 us
  local copies, waits for them, and re-layouts: 2.17 us -> 0 us
    pallas_call x2, Pallas kernels: 168 us -> 163 us  [the longest x1 141 us: local_step(): pl.pallas_call(comm_kernel, out_shape=(row, row, jax.ShapeDtypeStruct((2,...]
    unnamed x8 -> x0, local copies, waits for them, and re-layouts: 2.17 us -> none
where the time goes in v3:
time: 164 us
  Pallas kernels  163 us (99%)
    pallas_call x1, Pallas kernels, local_step(): pl.pallas_call(comm_kernel, out_shape=(row, row, jax.ShapeDtypeStruct((2,...  141 us
    pallas_call x1, Pallas kernels, local_step(): pl.pallas_call(wgrad_kernel, grid=(2 * NP,), out_shape=(row, row, jax.Sha...  22.4 us

profile of v3, /device:TPU:0, one launch (start us, length us, event | category | flops | bytes accessed | tf_op | source)
XLA Modules:
  0.0 163.6 jit_solution(11636748353924359407)
XLA Ops:
  0.6 140.6 %mlp_comm.1 = (bf16[8,3072]{1,0:T(8,128)(2,1)}, bf16[8,3072]{1,0:T(8,128)(2,1)}, bf16[2,128,384]{2,1,0:T(8,128)(2,1)}, bf16[8,2,2,2,2,3,16,768]{7,6,5,4,3,2,1,0:T(8,128)(2,1)}) custom-call(bf16[8,3072]{1,0:T(8,128)(2,1)} %x_ref.1, bf16[8,3072]{1,0:T(8,128)(2,1)} %gy_ref.1, bf16[384,12288]{1,0:T(8,128)(2,1)} %wg_hbm.1, bf16[384,12288]{1,0:T(8,128)(2,1)} %wu_hbm.1, ...), custom_call_target="tpu_custom_call" | custom-call | tf_op jit(solution)/shard_map/mlp_comm/pallas_call | solution.py:361
  141.2 22.4 %mlp_wgrad.1 = (bf16[8,3072]{1,0:T(8,128)(2,1)}, bf16[8,3072]{1,0:T(8,128)(2,1)}, f32[384,12288]{1,0:T(8,128)}, f32[384,12288]{1,0:T(8,128)}, f32[12288,384]{1,0:T(8,128)}) custom-call(bf16[2,128,384]{2,1,0:T(8,128)(2,1)} %get-tuple-element.9.xs_ref, bf16[8,2,2,2,2,3,16,768]{7,6,5,4,3,2,1,0:T(8,128)(2,1)} %get-tuple-element.10.g_ref, ...), custom_call_target="tpu_custom_call" | custom-call | tf_op jit(solution)/shard_map/mlp_wgrad/pallas_call | solution.py:394
